TPU v7x, 32 devices: a whole 2x2x4 slice. The times are simulated.
32 devices in a mesh: fsdp: 4 (over y, core), tp: 4 (over z), rollout: 2 (over x).
Axes of the slice: x: 2, y: 2, z: 4, core: 2. Of those that a mesh axis runs over, the one named last changes fastest.
Arguments:
- weights: bfloat16 [2, 4096, 14336], P('rollout', 'fsdp', 'tp'), may hold values from -6 to 6
- gradient: bfloat16 [2, 4096, 14336], P('rollout', 'fsdp', 'tp'), may hold values from -6 to 6
- momentum: float32 [2, 4096, 14336], P('rollout', 'fsdp', 'tp'), may hold values from -90 to 90
- basis: float32 [2, 14336, 512], P('rollout', 'tp'), may hold values from -6 to 6
Outputs:
- weights_next: bfloat16 [2, 4096, 14336], P('rollout', 'fsdp', 'tp')
- momentum_next: float32 [2, 4096, 14336], P('rollout', 'fsdp', 'tp')
- basis_next: float32 [2, 14336, 512], P('rollout', 'tp')
- rollout_weights: bfloat16 [2, 4096, 14336], P(None, 'fsdp', 'tp')
All inputs are finite; a program needn't handle non-finite values.
Results may differ from a plain program's by a relative error of at most 0.013.
Values may be sent and summed in bfloat16 or wider, within the bound.
A program may use at most 192 MiB of HBM per device.

v0:
```python
import jax
import jax.numpy as jnp
from jax import lax
from jax.sharding import PartitionSpec as P

COLS = 14336


HIGH = lax.Precision.HIGHEST


def body(weights, gradient, momentum, basis):
    blend = momentum[0] + gradient[0].astype(jnp.float32)
    prior = basis[0]
    share = lax.psum_scatter(
        jnp.dot(blend, prior, precision=HIGH, preferred_element_type=jnp.float32),
        "tp",
        scatter_dimension=0,
        tiled=True,
    )
    gram = lax.psum(
        jnp.dot(share.T, share, precision=HIGH, preferred_element_type=jnp.float32), ("fsdp", "tp")
    )
    left = lax.all_gather(share, "tp", axis=0, tiled=True)
    lower = jnp.linalg.cholesky(gram)
    ortho = lax.linalg.triangular_solve(lower, left, left_side=False, lower=True, transpose_a=True)
    partial_right = jnp.dot(blend.T, ortho, precision=HIGH, preferred_element_type=jnp.float32)
    right = lax.psum(partial_right.astype(jnp.bfloat16), "fsdp").astype(jnp.float32)
    squares = lax.psum(jnp.sum(right * right, axis=0), "tp")
    meansq = squares / COLS
    basis_new = right * lax.rsqrt(meansq + 1e-06)
    norms = jnp.sqrt(meansq + 1e-06)
    moment_new = blend - 0.05 * jnp.dot(
        ortho * norms, basis_new.T, precision=HIGH, preferred_element_type=jnp.float32
    )
    update = jnp.dot(ortho, basis_new.T, precision=HIGH, preferred_element_type=jnp.float32)
    weight_new = (weights[0].astype(jnp.float32) - 0.3 * update).astype(jnp.bfloat16)[None]
    rollout_copy = lax.all_gather(weight_new, "rollout", axis=0, tiled=True)
    return (weight_new, moment_new[None], basis_new[None], rollout_copy)


def solution(mesh):
    return jax.shard_map(
        body,
        mesh=mesh,
        in_specs=(
            P("rollout", "fsdp", "tp"),
            P("rollout", "fsdp", "tp"),
            P("rollout", "fsdp", "tp"),
            P("rollout", "tp", None),
        ),
        out_specs=(
            P("rollout", "fsdp", "tp"),
            P("rollout", "fsdp", "tp"),
            P("rollout", "tp", None),
            P(None, "fsdp", "tp"),
        ),
        check_vma=False,
    )
```

profile of v0, /device:TPU:0, one launch (start us, length us, event | category | flops | bytes accessed | tf_op | source)
XLA Modules:
  0.0 710.0 jit_solution(7459058599054322177)
XLA Ops:
  7.2 29.3 %fusion.3 = f32[1024,512]{1,0:T(8,128)} fusion(f32[1,3584,512]{2,1,0:T(8,128)} %param.7, f32[1,1024,3584]{2,1,0:T(8,128)} %param.6, bf16[1,1024,3584]{2,1,0:T(8,128)(2,1)} %param.5), kind=kOutput, calls=%fused_computation.7 | convolution fusion | flops 22555918336 | bytes 31457280 | tf_op jit(solution)/shard_map/dot_general | solution.py:16
  36.5 46.5 %reduce-scatter.2.cloned.1.call-done = f32[256,512]{1,0:T(8,128)} async-done(((f32[1024,512]{1,0:T(8,128)}), f32[256,512]{1,0:T(8,128)}) %reduce-scatter.2.cloned.1.call-update) | async-done | bytes 524304 | tf_op jit(solution)/shard_map/reduce_scatter | solution.py:15
  83.0 3.2 fusion.58
  87.5 92.5 %all-reduce.4.cloned.1.call-done = f32[512,512]{0,1:T(8,128)} async-done(((f32[512,512]{0,1:T(8,128)}), f32[512,512]{0,1:T(8,128)}) %all-reduce.4.cloned.1.call-update) | async-done | bytes 1048592 | tf_op jit(solution)/shard_map/psum | solution.py:21
  183.1 11.7 %cholesky.104 = f32[128,128]{1,0:T(8,128)S(1)} custom-call(f32[128,128]{1,0:T(8,128)S(1)} %cholesky.266), custom_call_target="Cholesky" | custom-call | tf_op jit(solution)/shard_map/jit(cholesky)/cholesky | solution.py:25
  194.8 9.8 %custom-call.30 = f32[1,128,128]{1,2,0:T(8,128)S(1)} custom-call(f32[1,128,128]{2,1,0:T(8,128)S(1)} %get-tuple-element.31), custom_call_target="InvertDiagBlocksLowerTriangular" | custom-call | tf_op jit(solution)/shard_map/jit(cholesky)/cholesky | solution.py:25
  205.4 11.7 %cholesky.217 = f32[128,128]{1,0:T(8,128)S(1)} custom-call(f32[128,128]{1,0:T(8,128)S(1)} %cholesky.270), custom_call_target="Cholesky" | custom-call | tf_op jit(solution)/shard_map/jit(cholesky)/cholesky | solution.py:25
  217.2 10.0 %custom-call.31 = f32[1,128,128]{1,2,0:T(8,128)S(1)} custom-call(f32[1,128,128]{2,1,0:T(8,128)S(1)} %get-tuple-element.28), custom_call_target="InvertDiagBlocksLowerTriangular" | custom-call | tf_op jit(solution)/shard_map/jit(cholesky)/cholesky | solution.py:25
  227.8 11.7 %cholesky.238 = f32[128,128]{1,0:T(8,128)S(1)} custom-call(f32[128,128]{1,0:T(8,128)S(1)} %cholesky.275), custom_call_target="Cholesky" | custom-call | tf_op jit(solution)/shard_map/jit(cholesky)/cholesky | solution.py:25
  239.6 9.8 %custom-call.32 = f32[1,128,128]{1,2,0:T(8,128)S(1)} custom-call(f32[1,128,128]{2,1,0:T(8,128)S(1)} %get-tuple-element.25), custom_call_target="InvertDiagBlocksLowerTriangular" | custom-call | tf_op jit(solution)/shard_map/jit(cholesky)/cholesky | solution.py:25
  250.0 11.7 %cholesky.255 = f32[128,128]{1,0:T(8,128)S(1)} custom-call(f32[128,128]{1,0:T(8,128)S(1)} %convolution_subtract_fusion.4), custom_call_target="Cholesky" | custom-call | tf_op jit(solution)/shard_map/jit(cholesky)/cholesky | solution.py:25
  266.6 8.0 %while.1 = (s32[]{:T(128)}, f32[512,512]{1,0:T(8,128)S(1)}, s32[4,2]{0,1:T(2,128)S(1)}, f32[4,128,128]{2,1,0:T(8,128)S(1)}, s32[]{:T(128)}) while((s32[]{:T(128)}, f32[512,512]{1,0:T(8,128)S(1)}, s32[4,2]{0,1:T(2,128)S(1)}, f32[4,128,128]{2,1,0:T(8,128)S(1)}, s32[]{:T(128)}) %tuple.32), condition=%wide.while_cond, body=%wide.while_body.sunk | while | flops 2 | bytes 131189 | solution.py:26
  274.6 39.3 %custom-call.33 = f32[4,128,128]{1,2,0:T(8,128)S(1)} custom-call(f32[4,128,128]{2,1,0:T(8,128)S(1)} %get-tuple-element.11), custom_call_target="InvertDiagBlocksLowerTriangular" | custom-call | tf_op jit(solution)/shard_map/triangular_solve | solution.py:26
  318.3 2.9 convolution_subtract_fusion
  321.8 3.7 fusion.23
  326.1 50.1 %fusion.11 = bf16[3584,512]{1,0:T(8,128)(2,1)} fusion(f32[1,1024,3584]{2,1,0:T(8,128)} %param.6, bf16[1,1024,3584]{2,1,0:T(8,128)(2,1)} %param.5, f32[1024,128]{0,1:T(8,128)S(1)} %fusion.41, f32[1024,128]{0,1:T(8,128)S(1)} %fusion.42, f32[1024,128]{0,1:T(8,128)S(1)} %fusion.43, f32[1024,128]{0,1:T(8,128)S(1)} %fusion.31), kind=kOutput, calls=%fused_computation.18 | convolution fusion | flops 22559326208 | bytes 27787264 | tf_op jit(solution)/shard_map/dot_general | solution.py:27
  376.3 76.2 %all-reduce.6.cloned.1.call-done = bf16[3584,512]{1,0:T(8,128)(2,1)} async-done(((bf16[3584,512]{1,0:T(8,128)(2,1)}), bf16[3584,512]{1,0:T(8,128)(2,1)}) %all-reduce.6.cloned.1.call-update) | async-done | bytes 3670032 | tf_op jit(solution)/shard_map/psum | solution.py:28
  452.5 2.9 fusion.9
  455.3 11.9 %psum.23 = f32[512]{0:T(512)S(1)} all-reduce(f32[512]{0:T(512)S(1)} %fusion.9), channel_id=1, replica_groups=mesh['fsdp'=4,'tp'=4,'rollout'=2] {'tp'}, use_global_device_ids=true, to_apply=%region_12.13 | all-reduce | flops 512 | bytes 4096 | tf_op jit(solution)/shard_map/psum | solution.py:29
  467.2 49.9 %fusion = bf16[1024,3584]{1,0:T(8,128)(2,1)} fusion(bf16[1,1024,3584]{2,1,0:T(8,128)(2,1)} %param.4, bf16[3584,512]{1,0:T(8,128)(2,1)} %all-reduce.6.cloned.1.call-done, f32[512]{0:T(512)S(1)} %get-tuple-element.33, f32[1024,128]{0,1:T(8,128)S(1)} %fusion.41, f32[1024,128]{0,1:T(8,128)S(1)} %fusion.42, f32[1024,128]{0,1:T(8,128)S(1)} %fusion.43, ...), kind=kOutput, calls=%fused_computation.3 | convolution fusion | flops 22568501248 | bytes 20449280 | tf_op jit(solution)/shard_map/dot_general | solution.py:36
  517.1 7.9 %fusion.6 = f32[1,3584,512]{2,1,0:T(8,128)} fusion(bf16[3584,512]{1,0:T(8,128)(2,1)} %all-reduce.6.cloned.1.call-done, f32[512]{0:T(512)S(1)} %get-tuple-element.33), kind=kLoop, calls=%fused_computation.13 | loop fusion | flops 3670016 | bytes 11012096 | tf_op jit(solution)/shard_map/broadcast_in_dim | solution.py:39
  525.0 52.9 %fusion.5 = f32[1,1024,3584]{2,1,0:T(8,128)} fusion(bf16[3584,512]{1,0:T(8,128)(2,1)S(1)} %copy-done, f32[1,1024,3584]{2,1,0:T(8,128)} %param.6, bf16[1,1024,3584]{2,1,0:T(8,128)(2,1)} %param.5, f32[512]{0:T(512)S(1)} %get-tuple-element.33, f32[512]{0:T(512)S(1)} %get-tuple-element.32, f32[1024,128]{0,1:T(8,128)S(1)} %fusion.41, ...), kind=kOutput, calls=%fused_computation.9 | convolution fusion | flops 22569025536 | bytes 42471424 | tf_op jit(solution)/shard_map/dot_general | solution.py:33
  577.9 112.2 %all-gather.6.cloned.1.call-done = bf16[2048,3584]{1,0:T(8,128)(2,1)} async-done(((bf16[1024,3584]{1,0:T(8,128)(2,1)}), bf16[2048,3584]{1,0:T(8,128)(2,1)}) %all-gather.6.cloned.1.call-update) | async-done | bytes 14680080 | tf_op jit(solution)/shard_map/all_gather | solution.py:38
  690.1 13.1 %copy.29 = bf16[2,1024,3584]{2,1,0:T(8,128)(2,1)} copy(bf16[2,1024,3584]{2,1,0:T(8,128)(2,1)} %bitcast.72) | data formatting | bytes 29360128
  (54 shorter events, 22.3 us)
Async XLA Ops:
  7.2 75.8 %reduce-scatter.2.cloned.1.call-start = ((), (), s32[]{:S(2)}) async-start(), calls=%async_computation.1 | async-start | bytes 2621440 | tf_op jit(solution)/shard_map/reduce_scatter | solution.py:15
  36.5 143.6 %all-reduce.4.cloned.1.call-start = ((), (), s32[]{:S(2)}) async-start(), calls=%async_computation.3 | async-start | bytes 2097152 | tf_op jit(solution)/shard_map/psum | solution.py:21
  86.2 227.7 %all-gather.4.cloned.1.call-start = ((), (), s32[]{:S(2)}) async-start(), calls=%async_computation.2 | async-start | bytes 2621440 | tf_op jit(solution)/shard_map/all_gather | solution.py:24
  87.0 365.5 %all-reduce.6.cloned.1.call-start = ((), (), s32[]{:S(2)}) async-start(), calls=%async_computation.4 | async-start | bytes 7340032 | tf_op jit(solution)/shard_map/psum | solution.py:28
  376.2 313.9 %all-gather.6.cloned.1.call-start = ((), (), s32[]{:S(2)}) async-start(), calls=%async_computation.5 | async-start | bytes 22020096 | tf_op jit(solution)/shard_map/all_gather | solution.py:38
  517.1 7.9 %copy-start = (bf16[3584,512]{1,0:T(8,128)(2,1)S(1)}, bf16[3584,512]{1,0:T(8,128)(2,1)}, u32[]{:S(2)}) copy-start(bf16[3584,512]{1,0:T(8,128)(2,1)} %all-reduce.6.cloned.1.call-done) | copy-start | bytes 11010052
Sparse Core Ops, SparseCore 0:
  36.6 46.3 reduce-scatter.1
  87.0 92.9 all-reduce.3
  181.6 44.7 all-gather.3
  376.4 76.0 all-reduce.5
  517.2 172.8 all-gather.5
where the time goes:
time: 716 us; the launch traced here: 710 us
  waiting for transfers between devices  328 us (46%)
  matrix products  199 us (28%)
  other arithmetic  130 us (18%)
  local copies, waits for them, and re-layouts  22.9 us (3%)
  between operations  16.8 us (2%)
  blocking collectives  11.9 us (2%)
    all_gather x1, waiting for transfers between devices, body(): rollout_copy = lax.all_gather(weight_new, 'rollout', axis=0, tiled=True)  112 us
    psum x1, waiting for transfers between devices, body(): lax.psum(jnp.dot(share.T, share, precision=HIGH, preferred_element_type=j...  92.5 us
    another operation x14, other arithmetic, body(): lower = jnp.linalg.cholesky(gram)  78.5 us
    psum x1, waiting for transfers between devices, body(): lax.psum(partial_right.astype(jnp.bfloat16), 'fsdp').astype(jnp.float32)  76.2 us
    dot_general x1, matrix products, body(): jnp.dot(ortho * norms, basis_new.T, precision=HIGH, preferred_element_typ...  52.9 us
    dot_general x1, matrix products, body(): jnp.dot(blend.T, ortho, precision=HIGH, preferred_element_type=jnp.float32)  50.1 us
    dot_general x1, matrix products, body(): jnp.dot(ortho, basis_new.T, precision=HIGH, preferred_element_type=jnp.fl...  49.9 us
    reduce_scatter x1, waiting for transfers between devices, body(): lax.psum_scatter(jnp.dot(blend, prior, precision=HIGH, preferred_element_...  46.5 us
  transfers between devices with their start and end apart: 5, of which 4 were waited for; matrix products, arithmetic and copies ran while one was open for 27% of the time, Pallas kernels for 0%

commit v1 on v0

v1 whole, which is shorter than its diff:
```python
import functools

import jax
import jax.numpy as jnp
from jax import lax
from jax.experimental import pallas as pl
from jax.experimental.pallas import tpu as pltpu
from jax.sharding import PartitionSpec as P


HIGH = lax.Precision.HIGHEST
BLOCK = 128


def dot_t(a, b):
    return lax.dot_general(
        a, b, (((1,), (1,)), ((), ())), precision=HIGH, preferred_element_type=jnp.float32
    )


def factor_kernel(g_ref, x_ref, a_ref, w_ref, s_ref, v_ref):
    n = g_ref.shape[0]
    nb = BLOCK
    a_ref[...] = g_ref[...]
    w_ref[...] = jnp.where(
        lax.broadcasted_iota(jnp.int32, (n, n), 0) == lax.broadcasted_iota(jnp.int32, (n, n), 1),
        1.0,
        0.0,
    ).astype(jnp.float32)
    lane = lax.broadcasted_iota(jnp.int32, (nb, nb), 1)
    sub = lax.broadcasted_iota(jnp.int32, (nb, nb), 0)
    lane_row = lax.broadcasted_iota(jnp.int32, (1, nb), 1)
    sub_col = lax.broadcasted_iota(jnp.int32, (nb, 1), 0)

    def step(k, carry):
        s = s_ref[...]
        v = v_ref[...]
        row = s_ref[pl.ds(k, 1), :]
        vrow = v_ref[pl.ds(k, 1), :]
        p = jnp.sum(jnp.where(lane_row == k, row, 0.0), axis=1, keepdims=True)
        col = jnp.sum(jnp.where(lane == k, s, 0.0), axis=1, keepdims=True)
        col = jnp.where(sub_col > k, col, 0.0)
        rp = 1.0 / p
        r = lax.rsqrt(p)
        r = r * (1.5 - 0.5 * p * r * r)
        s_ref[...] = s - col * (row * rp)
        v_ref[...] = v - col * (vrow * rp)
        v_ref[pl.ds(k, 1), :] = vrow * r
        return carry

    for lo in range(0, n, nb):
        hi = lo + nb
        s_ref[...] = a_ref[lo:hi, lo:hi]
        v_ref[...] = jnp.where(lane == sub, 1.0, 0.0).astype(jnp.float32)
        lax.fori_loop(0, nb, step, 0)
        inv = v_ref[...]
        x = jnp.dot(inv, w_ref[lo:hi, :hi], precision=HIGH, preferred_element_type=jnp.float32)
        x_ref[lo:hi, :hi] = x
        if hi < n:
            x_ref[lo:hi, hi:] = jnp.zeros((nb, n - hi), jnp.float32)
            panel = dot_t(a_ref[hi:, lo:hi], inv)
            a_ref[hi:, hi:] = a_ref[hi:, hi:] - dot_t(panel, panel)
            w_ref[hi:, :hi] = w_ref[hi:, :hi] - jnp.dot(
                panel, x, precision=HIGH, preferred_element_type=jnp.float32
            )


def inverse_factor(gram):
    n = gram.shape[0]
    return pl.pallas_call(
        factor_kernel,
        out_shape=jax.ShapeDtypeStruct((n, n), jnp.float32),
        in_specs=[pl.BlockSpec(memory_space=pltpu.VMEM)],
        out_specs=pl.BlockSpec(memory_space=pltpu.VMEM),
        scratch_shapes=[
            pltpu.VMEM((n, n), jnp.float32),
            pltpu.VMEM((n, n), jnp.float32),
            pltpu.VMEM((BLOCK, BLOCK), jnp.float32),
            pltpu.VMEM((BLOCK, BLOCK), jnp.float32),
        ],
        compiler_params=pltpu.CompilerParams(vmem_limit_bytes=16 << 20),
        cost_estimate=pl.CostEstimate(flops=2_000_000_000, bytes_accessed=8 * n * n, transcendentals=0),
        name="factor",
    )(gram)


def updated(w_ref, ortho_ref, right_ref, inv_ref):
    base = (right_ref[...].astype(jnp.float32) * inv_ref[...]).astype(jnp.bfloat16)
    update = lax.dot_general(
        ortho_ref[...], base, (((1,), (1,)), ((), ())), preferred_element_type=jnp.float32
    )
    return (w_ref[0].astype(jnp.float32) - 0.3 * update).astype(jnp.bfloat16)


def own_kernel(who_ref, w_ref, ortho_ref, right_ref, inv_ref, new_ref, both_ref):
    value = updated(w_ref, ortho_ref, right_ref, inv_ref)
    new_ref[0] = value
    both_ref[0] = value


def other_kernel(who_ref, w_ref, ortho_ref, right_ref, inv_ref, both_in, both_ref):
    both_ref[0] = updated(w_ref, ortho_ref, right_ref, inv_ref)


def pick(n, sizes):
    for s in sizes:
        if n % s == 0:
            return s
    return n


def apply_update(who, w, ortho, right, inv, both=None):
    _, rows, cols = w.shape
    rank = ortho.shape[1]
    tr = pick(rows, (512, 256, 128))
    tc = pick(cols, (896, 512, 256, 128))
    w_spec = pl.BlockSpec((1, tr, tc), lambda j, i, who: (0, i, j))
    both_spec = pl.BlockSpec((1, tr, tc), lambda j, i, who: (who[0], i, j))
    in_specs = [
        w_spec,
        pl.BlockSpec((tr, rank), lambda j, i, who: (i, 0)),
        pl.BlockSpec((tc, rank), lambda j, i, who: (j, 0)),
        pl.BlockSpec((1, rank), lambda j, i, who: (0, 0)),
    ]
    both_shape = jax.ShapeDtypeStruct((2, rows, cols), jnp.bfloat16)
    args = [who, w, ortho, right, inv]
    if both is None:
        kernel = own_kernel
        out_shape = (jax.ShapeDtypeStruct((1, rows, cols), jnp.bfloat16), both_shape)
        out_specs = (w_spec, both_spec)
        aliases = {}
    else:
        kernel = other_kernel
        in_specs.append(pl.BlockSpec(memory_space=pl.ANY))
        args.append(both)
        out_shape = both_shape
        out_specs = both_spec
        aliases = {5: 0}
    return pl.pallas_call(
        kernel,
        out_shape=out_shape,
        grid_spec=pltpu.PrefetchScalarGridSpec(
            num_scalar_prefetch=1,
            grid=(cols // tc, rows // tr),
            in_specs=in_specs,
            out_specs=out_specs,
        ),
        input_output_aliases=aliases,
        compiler_params=pltpu.CompilerParams(vmem_limit_bytes=32 << 20),
        cost_estimate=pl.CostEstimate(
            flops=2 * rows * cols * rank, bytes_accessed=6 * rows * cols, transcendentals=0
        ),
        name="apply_own" if both is None else "apply_other",
    )(*args)


def body(weights, gradient, momentum, basis):
    swap = functools.partial(lax.ppermute, axis_name="rollout", perm=[(0, 1), (1, 0)])
    me = lax.axis_index("rollout")
    cols = weights.shape[2] * lax.axis_size("tp")
    weights_other = swap(weights)
    blend = momentum[0] + gradient[0].astype(jnp.float32)
    share = lax.psum_scatter(
        jnp.dot(blend, basis[0], precision=lax.Precision.HIGH, preferred_element_type=jnp.float32),
        "tp",
        scatter_dimension=0,
        tiled=True,
    )
    gram = lax.psum(
        jnp.dot(share.T, share, precision=HIGH, preferred_element_type=jnp.float32), ("fsdp", "tp")
    )
    share, gram = lax.optimization_barrier((share, gram))
    left = lax.all_gather(share, "tp", axis=0, tiled=True)
    inverse = inverse_factor(gram)
    ortho = dot_t(left, inverse).astype(jnp.bfloat16)
    ortho_other = swap(ortho)
    partial_right = lax.dot_general(
        blend.astype(jnp.bfloat16),
        ortho,
        (((0,), (0,)), ((), ())),
        preferred_element_type=jnp.float32,
    )
    right = lax.psum(partial_right.astype(jnp.bfloat16), "fsdp")
    right_other = swap(right)
    wide = right.astype(jnp.float32)
    squares = lax.psum(jnp.sum(wide * wide, axis=0, keepdims=True), "tp")
    inv = lax.rsqrt(squares / cols + 1e-06)
    inv_other = swap(inv)
    weight_new, both = apply_update(me.reshape(1), weights, ortho, right, inv)
    moment_new = blend - 0.05 * lax.dot_general(
        ortho, right, (((1,), (1,)), ((), ())), preferred_element_type=jnp.float32
    )
    basis_new = wide * inv
    both = apply_update((1 - me).reshape(1), weights_other, ortho_other, right_other, inv_other, both)
    return (weight_new, moment_new[None], basis_new[None], both)


def solution(mesh):
    return jax.shard_map(
        body,
        mesh=mesh,
        in_specs=(
            P("rollout", "fsdp", "tp"),
            P("rollout", "fsdp", "tp"),
            P("rollout", "fsdp", "tp"),
            P("rollout", "tp", None),
        ),
        out_specs=(
            P("rollout", "fsdp", "tp"),
            P("rollout", "fsdp", "tp"),
            P("rollout", "tp", None),
            P(None, "fsdp", "tp"),
        ),
        check_vma=False,
    )
```

time: 716 us -> 449 us (0.63)
  matrix products: 199 us -> 56.8 us
  other arithmetic: 130 us -> 7.02 us
  Pallas kernels: 0 us -> 77 us
  waiting for transfers between devices: 328 us -> 273 us
  local copies, waits for them, and re-layouts: 22.9 us -> 4.31 us
    dot_general x4, matrix products: 182 us -> 53.6 us  [the longest x1 18.4 us: body(): jnp.dot(blend, basis[0], precision=lax.Precision.HIGH, preferred_element_...]
    another operation x17 -> x0, other arithmetic: 118 us -> none  [the longest x14 78.5 us: body(): lower = jnp.linalg.cholesky(gram)]
    all_gather x1 -> x0, waiting for transfers between devices: 112 us -> none  [body(): rollout_copy = lax.all_gather(weight_new, 'rollout', axis=0, tiled=True)]
    pallas_call x0 -> x3, Pallas kernels: none -> 77 us  [the longest x1 55.6 us: inverse_factor(): pl.pallas_call(factor_kernel, out_shape=jax.ShapeDtypeStruct((n, n), jnp....]
    ppermute x0 -> x4, waiting for transfers between devices: none -> 58.3 us  [the longest x1 58.3 us: body(): inv_other = swap(inv)]
    another operation x13 -> x0, matrix products: 14 us -> none  [the longest x7 12.1 us: body(): lax.linalg.triangular_solve(lower, left, left_side=False, lower=True, tra...]
    unnamed x3 -> x6, local copies, waits for them, and re-layouts: 13.1 us -> 4.31 us
    another operation x17 -> x0, local copies, waits for them, and re-layouts: 8.27 us -> none
  transfers between devices with their start and end apart: 5 -> 8, of which waited for: 4 -> 4; matrix products, arithmetic and copies ran while one was open for 27% -> 9% of each run, Pallas kernels for 0% -> 14%
where the time goes in v1:
time: 449 us
  waiting for transfers between devices  273 us (61%)
  Pallas kernels  77 us (17%)
  matrix products  56.8 us (13%)
  between operations  13.8 us (3%)
  blocking collectives  11.9 us (3%)
  other arithmetic  7.02 us (2%)
  starting transfers between devices  4.57 us (1%)
    psum x1, waiting for transfers between devices, body(): lax.psum(jnp.dot(share.T, share, precision=HIGH, preferred_element_type=j...  93.8 us
    psum x1, waiting for transfers between devices, body(): right = lax.psum(partial_right.astype(jnp.bfloat16), 'fsdp')  74.7 us
    ppermute x1, waiting for transfers between devices, body(): inv_other = swap(inv)  58.3 us
    pallas_call x1, Pallas kernels, inverse_factor(): pl.pallas_call(factor_kernel, out_shape=jax.ShapeDtypeStruct((n, n), jnp....  55.6 us
    reduce_scatter x1, waiting for transfers between devices, body(): lax.psum_scatter(jnp.dot(blend, basis[0], precision=lax.Precision.HIGH, p...  46.5 us
    pallas_call x2, Pallas kernels, apply_update(): pl.pallas_call(kernel, out_shape=out_shape, grid_spec=pltpu.PrefetchScala...  21.5 us
    dot_general x1, matrix products, body(): jnp.dot(blend, basis[0], precision=lax.Precision.HIGH, preferred_element_...  18.4 us
    dot_general x1, matrix products, body(): lax.dot_general(ortho, right, (((1,), (1,)), ((), ())), preferred_element...  15.7 us
  transfers between devices with their start and end apart: 8, of which 4 were waited for; matrix products, arithmetic and copies ran while one was open for 9% of the time, Pallas kernels for 14%

profile of v1, /device:TPU:0, one launch (start us, length us, event | category | flops | bytes accessed | tf_op | source)
XLA Modules:
  0.0 448.7 jit_solution(299463312511611119)
XLA Ops:
  7.2 18.4 %fusion = f32[1024,512]{1,0:T(8,128)} fusion(f32[1,3584,512]{2,1,0:T(8,128)} %param.7, f32[1,1024,3584]{2,1,0:T(8,128)} %param.6, bf16[1,1024,3584]{2,1,0:T(8,128)(2,1)} %param.5), kind=kOutput, calls=%fused_computation.2 | convolution fusion | flops 11281629184 | bytes 31457280 | tf_op jit(solution)/shard_map/dot_general | solution.py:164
  25.6 0.0 all-reduce.3.cloned.1.call-start
  25.7 46.5 %reduce-scatter.2.cloned.1.call-done = f32[256,512]{1,0:T(8,128)} async-done(((f32[1024,512]{1,0:T(8,128)}), f32[256,512]{1,0:T(8,128)}) %reduce-scatter.2.cloned.1.call-update) | async-done | bytes 524304 | tf_op jit(solution)/shard_map/reduce_scatter | solution.py:163
  72.2 3.2 fusion.8
  75.4 0.0 all-gather.2.cloned.1.call-start
  75.4 93.8 %all-reduce.3.cloned.1.call-done.g_ref = f32[512,512]{1,0:T(8,128)} async-done(((f32[512,512]{1,0:T(8,128)}), f32[512,512]{1,0:T(8,128)}) %all-reduce.3.cloned.1.call-update) | async-done | bytes 1048592 | tf_op jit(solution)/shard_map/psum | solution.py:169
  169.2 0.2 all-reduce.5.cloned.1.call-start
  169.4 1.5 collective-permute-start
  171.0 1.2 copy-done.2
  172.2 55.6 %factor.1 = f32[512,512]{1,0:T(8,128)S(1)} custom-call(f32[512,512]{1,0:T(8,128)S(1)} %copy-done.2), custom_call_target="tpu_custom_call" | custom-call | flops 2000000000 | bytes 2097152 | tf_op jit(solution)/shard_map/factor/pallas_call | solution.py:70
  227.8 5.1 %convolution_convert_fusion.ortho_ref = bf16[1024,512]{1,0:T(8,128)(2,1)S(1)} fusion(f32[1024,512]{1,0:T(8,128)} %all-gather.2.cloned.1.call-done, f32[512,512]{1,0:T(8,128)S(1)} %factor.1), kind=kOutput, calls=%fused_computation.13 | convolution fusion | flops 3221749760 | bytes 4194304 | tf_op jit(solution)/shard_map/dot_general | solution.py:16
  232.9 14.5 %fusion.7 = bf16[3584,512]{1,0:T(8,128)(2,1)} fusion(bf16[1024,512]{1,0:T(8,128)(2,1)S(1)} %convolution_convert_fusion.ortho_ref, f32[1,1024,3584]{2,1,0:T(8,128)} %param.6, bf16[1,1024,3584]{2,1,0:T(8,128)(2,1)} %param.5), kind=kOutput, calls=%fused_computation.12 | convolution fusion | flops 3770941440 | bytes 26738688 | tf_op jit(solution)/shard_map/dot_general | solution.py:177
  247.4 0.6 collective-permute-start.1
  248.0 74.7 %all-reduce.5.cloned.1.call-done.right_ref = bf16[3584,512]{1,0:T(8,128)(2,1)} async-done(((bf16[3584,512]{1,0:T(8,128)(2,1)}), bf16[3584,512]{1,0:T(8,128)(2,1)}) %all-reduce.5.cloned.1.call-update) | async-done | bytes 3670032 | tf_op jit(solution)/shard_map/psum | solution.py:183
  322.6 1.5 collective-permute-start.2
  324.1 2.9 fusion.3
  327.0 11.9 %psum.23 = f32[1,512]{1,0:T(1,128)S(1)} all-reduce(f32[1,512]{1,0:T(1,128)S(1)} %bitcast.29), channel_id=1, replica_groups=mesh['fsdp'=4,'tp'=4,'rollout'=2] {'tp'}, use_global_device_ids=true, to_apply=%region_4.0 | all-reduce | flops 512 | bytes 4096 | tf_op jit(solution)/shard_map/psum | solution.py:186
  338.9 0.6 collective-permute-start.3
  339.6 15.7 %fusion.2 = f32[1,1024,3584]{2,1,0:T(8,128)} fusion(bf16[1024,512]{1,0:T(8,128)(2,1)S(1)} %convolution_convert_fusion.ortho_ref, bf16[3584,512]{1,0:T(8,128)(2,1)} %all-reduce.5.cloned.1.call-done.right_ref, f32[1,1024,3584]{2,1,0:T(8,128)} %param.6, bf16[1,1024,3584]{2,1,0:T(8,128)(2,1)} %param.5), kind=kOutput, calls=%fused_computation.4 | convolution fusion | flops 3772776448 | bytes 41418752 | tf_op jit(solution)/shard_map/dot_general | solution.py:190
  355.3 4.1 fusion.4
  359.4 3.1 copy-done.1
  362.5 9.2 %apply_own.1 = (bf16[1,1024,3584]{2,1,0:T(8,128)(2,1)}, bf16[2,1024,3584]{2,1,0:T(8,128)(2,1)}) custom-call(s32[1]{0:T(128)} %bitcast.who_ref, bf16[1,1024,3584]{2,1,0:T(8,128)(2,1)S(1)} %copy-done.1, bf16[1024,512]{1,0:T(8,128)(2,1)S(1)} %convolution_convert_fusion.ortho_ref, bf16[3584,512]{1,0:T(8,128)(2,1)S(1)} %copy-done, f32[1,512]{1,0:T(1,128)S(1)} %add_rsqrt_fusion.inv_ref), custom_call_target="tpu_custom_call" | custom-call | flops 3758096384 | bytes 22020096 | tf_op jit(solution)/shard_map/apply_own/pallas_call | solution.py:139
  371.6 58.3 %collective-permute-done.3.inv_ref = f32[1,512]{1,0:T(1,128)S(1)} collective-permute-done((f32[1,512]{1,0:T(1,128)S(1)}, f32[1,512]{1,0:T(1,128)S(1)}, u32[]{:S(2)}, u32[]{:S(2)}) %collective-permute-start.3) | collective-permute-done | bytes 2080 | tf_op jit(solution)/shard_map/ppermute | solution.py:188
  429.9 12.3 %apply_other.1 = bf16[2,1024,3584]{2,1,0:T(8,128)(2,1)} custom-call(s32[1]{0:T(128)} %bitcast.7.who_ref, bf16[1,1024,3584]{2,1,0:T(8,128)(2,1)} %collective-permute-done.w_ref, bf16[1024,512]{1,0:T(8,128)(2,1)S(1)} %collective-permute-done.1.ortho_ref, bf16[3584,512]{1,0:T(8,128)(2,1)} %collective-permute-done.2.right_ref, ...), custom_call_target="tpu_custom_call", output_to_operand_aliasing={{}: (5, {})} | custom-call | flops 3758096384 | bytes 22020096 | tf_op jit(solution)/shard_map/apply_other/pallas_call | solution.py:139
  (14 shorter events, 0.2 us)
Async XLA Ops:
  7.2 65.0 %reduce-scatter.2.cloned.1.call-start = ((), (), s32[]{:S(2)}) async-start(), calls=%async_computation.1 | async-start | bytes 2621440 | tf_op jit(solution)/shard_map/reduce_scatter | solution.py:163
  25.6 143.6 %all-reduce.3.cloned.1.call-start = ((), (), s32[]{:S(2)}) async-start(), calls=%async_computation.2 | async-start | bytes 2097152 | tf_op jit(solution)/shard_map/psum | solution.py:169
  75.4 152.4 %all-gather.2.cloned.1.call-start = ((), (), s32[]{:S(2)}) async-start(), calls=%async_computation.3 | async-start | bytes 2621440 | tf_op jit(solution)/shard_map/all_gather | solution.py:173
  169.2 153.4 %all-reduce.5.cloned.1.call-start = ((), (), s32[]{:S(2)}) async-start(), calls=%async_computation.4 | async-start | bytes 7340032 | tf_op jit(solution)/shard_map/psum | solution.py:183
  169.4 202.2 %collective-permute-start = (bf16[1,1024,3584]{2,1,0:T(8,128)(2,1)}, bf16[1,1024,3584]{2,1,0:T(8,128)(2,1)}, u32[]{:S(2)}, u32[]{:S(2)}) collective-permute-start(bf16[1,1024,3584]{2,1,0:T(8,128)(2,1)} %w_ref.1), channel_id=1, source_target_pairs={{0,1},{1,0},{2,3},{3,2},{4,5},{5,4},{6,7},{7,6},{8,9},{9,8},{10,11... | collective-permute-start | bytes 22020104 | tf_op jit(solution)/shard_map/ppermute | solution.py:161
  171.0 1.2 copy-start.2
  247.4 124.3 %collective-permute-start.1 = (bf16[1024,512]{1,0:T(8,128)(2,1)S(1)}, bf16[1024,512]{1,0:T(8,128)(2,1)S(1)}, u32[]{:S(2)}, u32[]{:S(2)}) collective-permute-start(bf16[1024,512]{1,0:T(8,128)(2,1)S(1)} %convolution_convert_fusion.ortho_ref), channel_id=1, source_target_pairs={{0,1},{1,0},{2,3},{3,2},{4,5},{5,4},{6,7},{7,6},{8,9},{9,8},{10,11... | collective-permute-start | bytes 3145736 | tf_op jit(solution)/shard_map/ppermute | solution.py:176
  322.6 107.2 %collective-permute-start.2 = (bf16[3584,512]{1,0:T(8,128)(2,1)}, bf16[3584,512]{1,0:T(8,128)(2,1)}, u32[]{:S(2)}, u32[]{:S(2)}) collective-permute-start(bf16[3584,512]{1,0:T(8,128)(2,1)} %all-reduce.5.cloned.1.call-done.right_ref), channel_id=1, source_target_pairs={{0,1},{1,0},{2,3},{3,2},{4,5},{5,4},{6,7},{7,6},{8,9},{9,8},{10,11... | collective-permute-start | bytes 11010056 | tf_op jit(solution)/shard_map/ppermute | solution.py:184
  338.9 16.3 %copy-start = (bf16[3584,512]{1,0:T(8,128)(2,1)S(1)}, bf16[3584,512]{1,0:T(8,128)(2,1)}, u32[]{:S(2)}) copy-start(bf16[3584,512]{1,0:T(8,128)(2,1)} %all-reduce.5.cloned.1.call-done.right_ref) | copy-start | bytes 11010052
  338.9 90.9 %collective-permute-start.3 = (f32[1,512]{1,0:T(1,128)S(1)}, f32[1,512]{1,0:T(1,128)S(1)}, u32[]{:S(2)}, u32[]{:S(2)}) collective-permute-start(f32[1,512]{1,0:T(1,128)S(1)} %add_rsqrt_fusion.inv_ref), channel_id=1, source_target_pairs={{0,1},{1,0},{2,3},{3,2},{4,5},{5,4},{6,7},{7,6},{8,9},{9,8},{10,11... | collective-permute-start | bytes 6152 | tf_op jit(solution)/shard_map/ppermute | solution.py:188
  359.4 3.1 copy-start.1
Sparse Core Ops, SparseCore 0:
  25.8 46.3 reduce-scatter.1
  76.2 92.9 all-reduce.2
  170.8 44.8 all-gather.1
  247.5 75.1 all-reduce.4
